TPU v7x, 256 devices: a whole 4x4x8 slice. The times are simulated.
256 devices in a mesh: dp: 8 (over z_lo, core), ep: 32 (over x, y, z_hi).
Axes of the slice: x: 4, y: 4, z: 8 (z_hi: 2, z_lo: 4; z = z_hi * 4 + z_lo), core: 2. Of those that a mesh axis runs over, the one named last changes fastest.
Arguments:
- tokens: bfloat16 [32768, 7168], P(('dp', 'ep')), may hold values from -6 to 6
- out_grad: bfloat16 [32768, 7168], P(('dp', 'ep')), may hold values from -3 to 3
- expert_ids: int32 [32768, 8], P(('dp', 'ep')), may hold values from 0 to 255, as said below
- route_weights: bfloat16 [32768, 8], P(('dp', 'ep')), may hold values from 0.099609375 to 1
- gate_matrix: bfloat16 [7168, 8192], P('dp', 'ep'), may hold values from -0.0625 to 0.0625
- up_matrix: bfloat16 [7168, 8192], P('dp', 'ep'), may hold values from -0.0625 to 0.0625
- down_matrix: bfloat16 [7168, 8192], P('dp', 'ep'), may hold values from -0.125 to 0.125
Outputs:
- input_gradient: bfloat16 [32768, 7168], P(('dp', 'ep'))
- route_gradient: float32 [32768, 8], P(('dp', 'ep'))
- gate_gradient: bfloat16 [7168, 8192], P('dp', 'ep')
- up_gradient: bfloat16 [7168, 8192], P('dp', 'ep')
- down_gradient: bfloat16 [7168, 8192], P('dp', 'ep')
Inputs may be any that keep to these rules, and one draw needn't show every extreme that they name: `expert_ids`: each row names 8 different ids, 2 in each of 4 groups of 32 consecutive ids. In each aligned block of 4096 rows, one id that is a multiple of 64 is named by 8 or more rows of every aligned block of 128 rows inside it.
All inputs are finite; a program needn't handle non-finite values.
Results may differ from a plain program's by a relative error of at most 0.014.
Values may be sent and summed in bfloat16 or wider, within the bound.
No kernel may reach another device: no remote copies, remote signals or barrier semaphores. Data moves between devices by JAX's collectives and lax.ppermute only.
A program may use at most 128 MiB of HBM per device.

v0:
```python
import math
import jax
import jax.numpy as jnp
from jax import lax
from jax.sharding import PartitionSpec as P

ROUTED = 256
TOPK = 8
SLICES = 8
CAP = 8


def in_one_piece(arrays, axis, split_dim, concat_dim, along):
    widths = [math.prod(a.shape[along:]) for a in arrays]
    both = jnp.concatenate(
        [a.reshape(*a.shape[:along], w) for a, w in zip(arrays, widths)], axis=along
    )
    filled = lax.all_to_all(both, axis, split_axis=split_dim, concat_axis=concat_dim, tiled=True)
    tiles = jnp.split(filled, [sum(widths[:k]) for k in range(1, len(widths))], axis=along)
    return tuple(
        (b.reshape(*filled.shape[:along], *a.shape[along:]) for a, b in zip(arrays, tiles))
    )


def hidden_terms(gate_pre, up_pre, projected, gate_rows):
    sigmoid = jax.nn.sigmoid(gate_pre)
    swished = gate_pre * sigmoid
    hidden = lax.optimization_barrier((swished * up_pre).astype(jnp.bfloat16)).astype(jnp.float32)
    route_part = jnp.sum(hidden * projected, axis=1).astype(jnp.bfloat16)
    scaling = gate_rows.astype(jnp.float32)[:, None]
    grad_hidden = scaling * projected
    gate_delta = grad_hidden * up_pre * sigmoid * (1.0 + gate_pre * (1.0 - sigmoid))
    up_delta = grad_hidden * swished
    deltas = jnp.concatenate([gate_delta, up_delta], axis=1).astype(jnp.bfloat16)
    scaled = (scaling * hidden).astype(jnp.bfloat16)
    return (deltas, scaled, route_part)


def body(tokens, out_grad, expert_ids, route_weights, gate_matrix, up_matrix, down_matrix):
    senders = lax.axis_size("ep")
    experts = senders // SLICES
    stride = ROUTED // experts
    tok_rows = tokens.shape[0]
    width = tokens.shape[1]
    hid_width = gate_matrix.shape[1]
    flat_ids = expert_ids.reshape(tok_rows * TOPK)
    window = flat_ids % stride == 0
    expert = jnp.where(window, flat_ids // stride, experts)
    column = jnp.arange(experts, dtype=jnp.int32)
    onehot = (expert[:, None] == column[None, :]).astype(jnp.int32)
    earlier = jnp.cumsum(onehot, axis=0) - onehot
    slot_index = jnp.sum(earlier * onehot, axis=1)
    kept_entry = window & (slot_index < CAP)
    places = jnp.arange(experts * CAP, dtype=jnp.int32)
    assign = kept_entry[:, None] & ((expert * CAP + slot_index)[:, None] == places[None, :])
    assign = assign.astype(jnp.float32).reshape(tok_rows, TOPK, experts * CAP)
    select = jnp.sum(assign, axis=1).astype(jnp.bfloat16)
    slot_in = jnp.einsum("ts,td->sd", select, tokens, preferred_element_type=jnp.float32).astype(
        jnp.bfloat16
    )
    slot_grad = jnp.einsum(
        "ts,td->sd", select, out_grad, preferred_element_type=jnp.float32
    ).astype(jnp.bfloat16)
    slot_gate = jnp.einsum("tks,tk->s", assign, route_weights.astype(jnp.float32)).astype(
        jnp.bfloat16
    )
    send_in = jnp.repeat(slot_in.reshape(experts, CAP, width), SLICES, axis=0)
    send_grad = jnp.repeat(slot_grad.reshape(experts, CAP, width), SLICES, axis=0)
    send_gate = jnp.repeat(slot_gate.reshape(experts, CAP), SLICES, axis=0)
    rows_in, rows_grad, rows_gate = in_one_piece((send_in, send_grad, send_gate), "ep", 0, 0, 2)
    total_rows = senders * CAP
    rows_in = rows_in.reshape(total_rows, width)
    rows_grad = rows_grad.reshape(total_rows, width)
    rows_gate = rows_gate.reshape(total_rows)
    stacked = jnp.concatenate([gate_matrix, up_matrix], axis=1)
    full_pair, full_down = (
        lax.all_gather(stacked, "dp", axis=0, tiled=True),
        lax.all_gather(down_matrix, "dp", axis=0, tiled=True),
    )
    gate_up = jnp.dot(rows_in, full_pair, preferred_element_type=jnp.float32)
    projected = jnp.dot(rows_grad, full_down, preferred_element_type=jnp.float32)
    deltas, scaled, route_part = hidden_terms(
        gate_up[:, :hid_width], gate_up[:, hid_width:], projected, rows_gate
    )
    partial_value = jnp.einsum(
        "rh,dh->rd", deltas, full_pair, preferred_element_type=jnp.float32
    ).astype(jnp.bfloat16)
    left = jnp.einsum("rd,rh->dh", rows_in, deltas, preferred_element_type=jnp.float32)
    right = jnp.einsum("rd,rh->dh", rows_grad, scaled, preferred_element_type=jnp.float32)
    summed = lax.psum_scatter(
        jnp.concatenate([left, right], axis=1).astype(jnp.bfloat16),
        "dp",
        scatter_dimension=0,
        tiled=True,
    ).astype(jnp.float32)
    back_in, back_route = in_one_piece(
        (partial_value.reshape(senders, CAP, width), route_part.reshape(senders, CAP)),
        "ep",
        0,
        0,
        2,
    )
    slot_sums = jnp.sum(
        back_in.reshape(experts, SLICES, CAP, width).astype(jnp.float32), axis=1
    ).reshape(experts * CAP, width)
    route_sums = jnp.sum(
        back_route.reshape(experts, SLICES, CAP).astype(jnp.float32), axis=1
    ).reshape(experts * CAP)
    input_gradient = jnp.dot(select.astype(jnp.float32), slot_sums).astype(jnp.bfloat16)
    route_gradient = jnp.einsum("tks,s->tk", assign, route_sums)
    gate_gradient = summed[:, :hid_width].astype(jnp.bfloat16)
    up_gradient = summed[:, hid_width : 2 * hid_width].astype(jnp.bfloat16)
    down_gradient = summed[:, 2 * hid_width :].astype(jnp.bfloat16)
    return (input_gradient, route_gradient, gate_gradient, up_gradient, down_gradient)


def solution(mesh):
    return jax.shard_map(
        body,
        mesh=mesh,
        in_specs=(
            P(("dp", "ep"), None),
            P(("dp", "ep"), None),
            P(("dp", "ep"), None),
            P(("dp", "ep"), None),
            P("dp", "ep"),
            P("dp", "ep"),
            P("dp", "ep"),
        ),
        out_specs=(
            P(("dp", "ep"), None),
            P(("dp", "ep"), None),
            P("dp", "ep"),
            P("dp", "ep"),
            P("dp", "ep"),
        ),
        check_vma=False,
    )
```

profile of v0, /device:TPU:2, one launch (start us, length us, event | category | flops | bytes accessed | tf_op | source)
XLA Modules:
  0.0 537.9 jit_solution(14116264508713704503)
XLA Ops:
  7.2 2.3 pad_maximum_fusion.3
  9.5 0.8 copy.124
  10.3 0.1 reshape.211
  10.4 0.1 reshape.210
  10.5 1.1 reduce-window.6
  11.7 0.2 slice_reduce_fusion
  11.9 0.2 reduce-window.9
  12.2 0.1 reduce_sum.48
  12.3 0.7 compare_and_fusion
  13.1 0.7 fusion.33
  13.7 0.8 fusion.5
  14.6 0.1 reshape.217
  14.7 0.1 copy.128
  14.8 0.1 reshape_reshape.2
  14.9 0.2 copy.129
  15.1 0.4 fusion.2
  15.5 1.9 fusion.1
  17.4 0.4 broadcast_in_dim.27
  17.8 0.4 broadcast_in_dim.26
  18.2 3.5 pad_maximum_fusion.1
  21.7 14.3 %all-to-all-start = ((bf16[32,8,14337]{2,1,0:T(8,128)(2,1)}), bf16[32,8,14337]{2,1,0:T(8,128)(2,1)}, u32[]{:S(2)}, u32[]{:S(2)}) async-start(bf16[32,8,14337]{2,1,0:T(8,128)(2,1)} %pad_maximum_fusion.1), calls=%async_computation | async-start | bytes 14811136 | tf_op jit(solution)/shard_map/all_to_all | solution.py:18
  36.1 0.7 all-gather.3.cloned.1.call-update
  36.8 0.2 reduce-scatter.4.cloned.1.call-start
  37.0 225.5 %all-to-all-done = bf16[32,8,14337]{2,1,0:T(8,128)(2,1)} async-done(((bf16[32,8,14337]{2,1,0:T(8,128)(2,1)}), bf16[32,8,14337]{2,1,0:T(8,128)(2,1)}, u32[]{:S(2)}, u32[]{:S(2)}) %all-to-all-start) | async-done | bytes 7340576 | tf_op jit(solution)/shard_map/all_to_all | solution.py:18
  262.5 0.9 convert_reduce_fusion.1
  263.4 0.1 reshape.223
  263.6 7.3 %fusion.4 = f32[256,512]{0,1:T(8,128)S(1)} fusion(bf16[7168,512]{1,0:T(8,128)(2,1)} %all-gather.5.cloned.1.call-done, bf16[32,8,14337]{2,1,0:T(8,128)(2,1)} %all-to-all-done), kind=kOutput, calls=%fused_computation.16 | convolution fusion | flops 1879048192 | bytes 11534336 | tf_op jit(solution)/shard_map/dot_general | solution.py:80
  270.8 22.5 %all-gather.3.cloned.1.call-done = bf16[7168,256]{1,0:T(8,128)(2,1)} async-done(((bf16[896,256]{1,0:T(8,128)(2,1)}), bf16[7168,256]{1,0:T(8,128)(2,1)}) %all-gather.3.cloned.1.call-update) | async-done | bytes 3670032 | tf_op jit(solution)/shard_map/all_gather | solution.py:78
  293.3 4.7 multiply_convert_fusion.2
  298.0 3.2 convolution_convert_fusion.1
  301.2 4.1 convolution_convert_fusion
  305.3 7.8 %pad_maximum_fusion = bf16[7168,768]{0,1:T(8,128)(2,1)} fusion(bf16[7168,256]{0,1:T(8,128)(2,1)S(1)} %convolution_convert_fusion.1, bf16[7168,512]{0,1:T(8,128)(2,1)S(1)} %convolution_convert_fusion), kind=kLoop, calls=%fused_computation | loop fusion | flops 22020096 | bytes 22020096 | tf_op jit(solution)/shard_map/concatenate | solution.py:91
  313.1 14.7 %copy.141 = bf16[7168,768]{1,0:T(8,128)(2,1)} copy(bf16[7168,768]{0,1:T(8,128)(2,1)} %pad_maximum_fusion) | data formatting | bytes 22020096
  327.9 0.2 convert_element_type.108
  328.2 5.2 fusion
  333.4 0.3 pad_maximum_fusion.2
  333.7 140.2 %all_to_all.10 = bf16[32,8,7169]{2,1,0:T(8,128)(2,1)S(1)} all-to-all(bf16[32,8,7169]{2,1,0:T(8,128)(2,1)S(1)} %pad_maximum_fusion.2), channel_id=1, replica_groups=mesh['dp'=8,'ep'=32] {'ep'}, dimensions={0} | all-to-all | bytes 7341056 | tf_op jit(solution)/shard_map/all_to_all | solution.py:18
  473.9 1.9 copy-done.2
  475.8 0.1 copy.143
  476.0 0.1 reshape.225
  476.0 0.1 reduce_sum.52
  476.1 0.1 copy.134
  476.2 0.1 reshape.228
  476.3 0.7 fusion.18
  477.1 2.6 convert_reduce_fusion
  479.7 1.9 convolution_convert_fusion.3
  481.6 47.4 %reduce-scatter.4.cloned.1.call-done = bf16[896,768]{1,0:T(8,128)(2,1)} async-done(((bf16[7168,768]{1,0:T(8,128)(2,1)}), bf16[896,768]{1,0:T(8,128)(2,1)}) %reduce-scatter.4.cloned.1.call-update) | async-done | bytes 1376272
  529.0 2.4 fusion.46
  (20 shorter events, 0.5 us)
Async XLA Ops:
  7.2 8.0 %copy-start = (bf16[128,7168]{1,0:T(8,128)(2,1)S(1)}, bf16[128,7168]{1,0:T(8,128)(2,1)}, u32[]{:S(2)}) copy-start(bf16[128,7168]{1,0:T(8,128)(2,1)} %param.8) | copy-start | bytes 5505028
  7.2 256.4 %all-gather.5.cloned.1.call-start = ((), (), s32[]{:S(2)}) async-start(), calls=%async_computation.4 | async-start | bytes 8257536 | tf_op jit(solution)/shard_map/all_gather | solution.py:77
  21.7 240.7 %all-to-all-start = ((bf16[32,8,14337]{2,1,0:T(8,128)(2,1)}), bf16[32,8,14337]{2,1,0:T(8,128)(2,1)}, u32[]{:S(2)}, u32[]{:S(2)}) async-start(bf16[32,8,14337]{2,1,0:T(8,128)(2,1)} %pad_maximum_fusion.1), calls=%async_computation | async-start | bytes 14811136 | tf_op jit(solution)/shard_map/all_to_all | solution.py:18
  36.0 257.2 %all-gather.3.cloned.1.call-start = ((), (), s32[]{:S(2)}) async-start(), calls=%async_computation.3 | async-start | bytes 4128768 | tf_op jit(solution)/shard_map/all_gather | solution.py:78
  36.8 492.2 %reduce-scatter.4.cloned.1.call-start = ((), (), s32[]{:S(2)}) async-start(), calls=%async_computation.5 | async-start | bytes 12386304
  333.4 198.0 %copy-start.1 = (bf16[128,7168]{1,0:T(8,128)(2,1)S(1)}, bf16[128,7168]{1,0:T(8,128)(2,1)}, u32[]{:S(2)}) copy-start(bf16[128,7168]{1,0:T(8,128)(2,1)} %param.8) | copy-start | bytes 5505028
  473.9 1.9 copy-start.2
Sparse Core Ops, SparseCore 0:
  10.4 200.9 all-gather.4
  213.2 80.0 all-gather.2
  328.0 200.9 reduce-scatter.3
where the time goes:
time: 539 us; the launch traced here: 538 us
  waiting for transfers between devices  296 us (55%)
  blocking collectives  140 us (26%)
  matrix products  30.2 us (6%)
  local copies, waits for them, and re-layouts  22.4 us (4%)
  other arithmetic  20.5 us (4%)
  starting transfers between devices  14.6 us (3%)
  between operations  13.9 us (3%)
    all_to_all x1, waiting for transfers between devices, in_one_piece(): lax.all_to_all(both, axis, split_axis=split_dim, concat_axis=concat_dim,...  225 us
    all_to_all x1, blocking collectives, in_one_piece(): lax.all_to_all(both, axis, split_axis=split_dim, concat_axis=concat_dim,...  140 us
    unnamed x4, waiting for transfers between devices  48.1 us
    all_gather x1, waiting for transfers between devices, body(): lax.all_gather(down_matrix, 'dp', axis=0, tiled=True)  22.5 us
    unnamed x9, local copies, waits for them, and re-layouts  17.6 us
    all_to_all x1, starting transfers between devices, in_one_piece(): lax.all_to_all(both, axis, split_axis=split_dim, concat_axis=concat_dim,...  14.3 us
  transfers between devices with their start and end apart: 4, of which 3 were waited for; matrix products, arithmetic and copies ran while one was open for 6% of the time, Pallas kernels for 0%

commit v1 on v0

--- a/solution.py
+++ b/solution.py
@@ -8,6 +8,12 @@
 TOPK = 8
 SLICES = 8
 CAP = 8
+
+
+def load_slabs_on(z):
+    return jnp.concatenate(
+        lax.all_to_all(jnp.stack([z] * lax.axis_size("dp"), axis=0), "dp", 0, 0), 0
+    )
 
 
 def in_one_piece(arrays, axis, split_dim, concat_dim, along):
@@ -75,7 +81,7 @@
     stacked = jnp.concatenate([gate_matrix, up_matrix], axis=1)
     full_pair, full_down = (
         lax.all_gather(stacked, "dp", axis=0, tiled=True),
-        lax.all_gather(down_matrix, "dp", axis=0, tiled=True),
+        load_slabs_on(down_matrix),
     )
     gate_up = jnp.dot(rows_in, full_pair, preferred_element_type=jnp.float32)
     projected = jnp.dot(rows_grad, full_down, preferred_element_type=jnp.float32)

time: 539 us -> 604 us (1.12)
  waiting for transfers between devices: 296 us -> 345 us
  starting transfers between devices: 14.6 us -> 31.8 us
    all_to_all x0 -> x1, waiting for transfers between devices: none -> 74.4 us  [load_slabs_on(): lax.all_to_all(jnp.stack([z] * lax.axis_size('dp'), axis=0), 'dp', 0, 0)]
    all_gather x1 -> x0, waiting for transfers between devices: 22.5 us -> none  [body(): lax.all_gather(down_matrix, 'dp', axis=0, tiled=True)]
    all_to_all x0 -> x1, starting transfers between devices: none -> 17.1 us  [load_slabs_on(): lax.all_to_all(jnp.stack([z] * lax.axis_size('dp'), axis=0), 'dp', 0, 0)]
    unnamed x4 -> x3, waiting for transfers between devices: 48.1 us -> 47.9 us
    unnamed x9 -> x15, local copies, waits for them, and re-layouts: 17.6 us -> 17.7 us
  transfers between devices with their start and end apart: 4 -> 4, of which waited for: 3 -> 3; matrix products, arithmetic and copies ran while one was open for 6% -> 4% of each run, Pallas kernels for 0% -> 0%
where the time goes in v1:
time: 604 us; the launch traced here: 603 us
  waiting for transfers between devices  345 us (57%)
  blocking collectives  138 us (23%)
  starting transfers between devices  31.8 us (5%)
  matrix products  30.1 us (5%)
  local copies, waits for them, and re-layouts  24.7 us (4%)
  other arithmetic  19.3 us (3%)
  between operations  14.3 us (2%)
    all_to_all x1, waiting for transfers between devices, in_one_piece(): lax.all_to_all(both, axis, split_axis=split_dim, concat_axis=concat_dim,...  222 us
    all_to_all x1, blocking collectives, in_one_piece(): lax.all_to_all(both, axis, split_axis=split_dim, concat_axis=concat_dim,...  138 us
    all_to_all x1, waiting for transfers between devices, load_slabs_on(): lax.all_to_all(jnp.stack([z] * lax.axis_size('dp'), axis=0), 'dp', 0, 0)  74.4 us
    unnamed x3, waiting for transfers between devices  47.9 us
    unnamed x15, local copies, waits for them, and re-layouts  17.7 us
    all_to_all x1, starting transfers between devices, load_slabs_on(): lax.all_to_all(jnp.stack([z] * lax.axis_size('dp'), axis=0), 'dp', 0, 0)  17.1 us
    all_to_all x1, starting transfers between devices, in_one_piece(): lax.all_to_all(both, axis, split_axis=split_dim, concat_axis=concat_dim,...  14.4 us
  transfers between devices with their start and end apart: 4, of which 3 were waited for; matrix products, arithmetic and copies ran while one was open for 4% of the time, Pallas kernels for 0%

profile of v1, /device:TPU:2, one launch (start us, length us, event | category | flops | bytes accessed | tf_op | source)
XLA Modules:
  0.0 603.0 jit_solution(15357875025925203012)
XLA Ops:
  7.2 0.9 copy.124
  8.1 0.1 reshape.216
  8.2 0.1 reshape.215
  8.3 1.1 reduce-window.6
  9.5 0.2 slice_reduce_fusion
  9.7 0.2 reduce-window.9
  10.1 0.7 compare_and_fusion
  10.9 0.7 fusion.33
  11.6 0.8 fusion.5
  12.4 0.1 reshape.222
  12.5 0.1 copy.128
  12.7 0.1 reshape_reshape.2
  12.8 0.2 copy.129
  12.9 0.4 fusion.2
  13.3 1.9 fusion.1
  15.2 0.4 broadcast_in_dim.26
  15.6 0.4 broadcast_in_dim.27
  16.0 3.5 pad_maximum_fusion.1
  19.5 14.4 %all-to-all-start = ((bf16[32,8,14337]{2,1,0:T(8,128)(2,1)}), bf16[32,8,14337]{2,1,0:T(8,128)(2,1)}, u32[]{:S(2)}, u32[]{:S(2)}) async-start(bf16[32,8,14337]{2,1,0:T(8,128)(2,1)} %pad_maximum_fusion.1), calls=%async_computation | async-start | bytes 14811136 | tf_op jit(solution)/shard_map/all_to_all | solution.py:24
  34.1 1.0 pad_maximum_fusion.3
  35.1 222.3 %all-to-all-done = bf16[32,8,14337]{2,1,0:T(8,128)(2,1)} async-done(((bf16[32,8,14337]{2,1,0:T(8,128)(2,1)}), bf16[32,8,14337]{2,1,0:T(8,128)(2,1)}, u32[]{:S(2)}, u32[]{:S(2)}) %all-to-all-start) | async-done | bytes 7340576 | tf_op jit(solution)/shard_map/all_to_all | solution.py:24
  257.4 2.1 stack.2
  259.5 17.1 %all-to-all-start.1 = ((bf16[8,896,256]{2,1,0:T(8,128)(2,1)}), bf16[8,896,256]{2,1,0:T(8,128)(2,1)}, u32[]{:S(2)}, u32[]{:S(2)}) async-start(bf16[8,896,256]{2,1,0:T(8,128)(2,1)} %stack.2), calls=%async_computation.1 | async-start | bytes 7340032 | tf_op jit(solution)/shard_map/all_to_all | solution.py:15
  276.6 0.2 reduce-scatter.4.cloned.1.call-start
  276.8 0.9 convert_reduce_fusion.1
  277.8 0.1 reshape.229
  277.9 7.2 %fusion.4 = f32[256,512]{0,1:T(8,128)S(1)} fusion(bf16[7168,512]{1,0:T(8,128)(2,1)} %all-gather.2.cloned.1.call-done, bf16[32,8,14337]{2,1,0:T(8,128)(2,1)} %all-to-all-done), kind=kOutput, calls=%fused_computation.16 | convolution fusion | flops 1879048192 | bytes 11534336 | tf_op jit(solution)/shard_map/dot_general | solution.py:86
  285.1 74.4 %all-to-all-done.1 = bf16[8,896,256]{2,1,0:T(8,128)(2,1)} async-done(((bf16[8,896,256]{2,1,0:T(8,128)(2,1)}), bf16[8,896,256]{2,1,0:T(8,128)(2,1)}, u32[]{:S(2)}, u32[]{:S(2)}) %all-to-all-start.1) | async-done | bytes 3670048 | tf_op jit(solution)/shard_map/all_to_all | solution.py:15
  359.5 4.7 multiply_convert_fusion.2
  364.2 3.2 convolution_convert_fusion.1
  367.4 4.1 convolution_convert_fusion
  371.5 7.8 %pad_maximum_fusion = bf16[7168,768]{0,1:T(8,128)(2,1)} fusion(bf16[7168,256]{0,1:T(8,128)(2,1)S(1)} %convolution_convert_fusion.1, bf16[7168,512]{0,1:T(8,128)(2,1)S(1)} %convolution_convert_fusion), kind=kLoop, calls=%fused_computation | loop fusion | flops 22020096 | bytes 22020096 | tf_op jit(solution)/shard_map/concatenate | solution.py:97
  379.3 14.7 %copy.141 = bf16[7168,768]{1,0:T(8,128)(2,1)} copy(bf16[7168,768]{0,1:T(8,128)(2,1)} %pad_maximum_fusion) | data formatting | bytes 22020096
  394.1 0.2 convert_element_type.108
  394.4 5.2 fusion
  399.6 0.3 pad_maximum_fusion.2
  399.8 138.3 %all_to_all.15 = bf16[32,8,7169]{2,1,0:T(8,128)(2,1)S(1)} all-to-all(bf16[32,8,7169]{2,1,0:T(8,128)(2,1)S(1)} %pad_maximum_fusion.2), channel_id=1, replica_groups=mesh['dp'=8,'ep'=32] {'ep'}, dimensions={0} | all-to-all | bytes 7341056 | tf_op jit(solution)/shard_map/all_to_all | solution.py:24
  538.1 1.9 copy-done.2
  540.0 0.1 copy.143
  540.2 0.1 reshape.231
  540.3 0.1 reduce_sum.52
  540.4 0.1 copy.134
  540.5 0.1 reshape.234
  540.5 0.7 fusion.18
  541.3 2.7 convert_reduce_fusion
  544.0 1.9 convolution_convert_fusion.3
  545.9 47.9 %reduce-scatter.4.cloned.1.call-done = bf16[896,768]{1,0:T(8,128)(2,1)} async-done(((bf16[7168,768]{1,0:T(8,128)(2,1)}), bf16[896,768]{1,0:T(8,128)(2,1)}) %reduce-scatter.4.cloned.1.call-update) | async-done | bytes 1376272
  593.8 2.4 fusion.46
  (26 shorter events, 0.6 us)
Async XLA Ops:
  7.2 5.8 copy-start
  19.5 14.5 %copy-start.3 = (bf16[896,256]{1,0:T(8,128)(2,1)S(1)}, bf16[896,256]{1,0:T(8,128)(2,1)}, u32[]{:S(2)}) copy-start(bf16[896,256]{1,0:T(8,128)(2,1)} %param.12) | copy-start | bytes 1376260
  19.5 14.5 %copy-start.4 = (bf16[896,256]{1,0:T(8,128)(2,1)S(1)}, bf16[896,256]{1,0:T(8,128)(2,1)}, u32[]{:S(2)}) copy-start(bf16[896,256]{1,0:T(8,128)(2,1)} %param.11) | copy-start | bytes 1376260
  19.5 237.8 %copy-start.5 = (bf16[896,256]{1,0:T(8,128)(2,1)S(1)}, bf16[896,256]{1,0:T(8,128)(2,1)}, u32[]{:S(2)}) copy-start(bf16[896,256]{1,0:T(8,128)(2,1)} %param.13) | copy-start | bytes 1376260
  19.5 237.8 %all-to-all-start = ((bf16[32,8,14337]{2,1,0:T(8,128)(2,1)}), bf16[32,8,14337]{2,1,0:T(8,128)(2,1)}, u32[]{:S(2)}, u32[]{:S(2)}) async-start(bf16[32,8,14337]{2,1,0:T(8,128)(2,1)} %pad_maximum_fusion.1), calls=%async_computation | async-start | bytes 14811136 | tf_op jit(solution)/shard_map/all_to_all | solution.py:24
  34.0 243.9 %all-gather.2.cloned.1.call-start = ((), (), s32[]{:S(2)}) async-start(), calls=%async_computation.4 | async-start | bytes 8257536 | tf_op jit(solution)/shard_map/all_gather | solution.py:83
  259.5 100.0 %all-to-all-start.1 = ((bf16[8,896,256]{2,1,0:T(8,128)(2,1)}), bf16[8,896,256]{2,1,0:T(8,128)(2,1)}, u32[]{:S(2)}, u32[]{:S(2)}) async-start(bf16[8,896,256]{2,1,0:T(8,128)(2,1)} %stack.2), calls=%async_computation.1 | async-start | bytes 7340032 | tf_op jit(solution)/shard_map/all_to_all | solution.py:15
  276.6 317.1 %reduce-scatter.4.cloned.1.call-start = ((), (), s32[]{:S(2)}) async-start(), calls=%async_computation.5 | async-start | bytes 12386304
  399.6 196.6 %copy-start.1 = (bf16[128,7168]{1,0:T(8,128)(2,1)S(1)}, bf16[128,7168]{1,0:T(8,128)(2,1)}, u32[]{:S(2)}) copy-start(bf16[128,7168]{1,0:T(8,128)(2,1)} %param.8) | copy-start | bytes 5505028
  538.1 1.9 copy-start.2
Sparse Core Ops, SparseCore 0:
  37.2 218.7 all-gather.1
  394.2 199.5 reduce-scatter.3
